TPU v7x, 32 devices: a whole 2x2x4 slice. The times are simulated.
32 devices in a mesh: gx: 8 (over z, x), ma: 4 (over y, core).
Axes of the slice: x: 2, y: 2, z: 4, core: 2. Of those that a mesh axis runs over, the one named last changes fastest.
Arguments:
- recorded: float32 [4096, 128, 128], P('ma', 'gx'), may hold values from -51 to 51
- kernel: bfloat16 [2, 8, 4096, 4096], P(None, 'gx', 'ma'), may hold values from -1 to 1
- freq_bins: int32 [8], replicated, may hold values from 1 to 63
- window_start: int32 [4096, 128], P('ma', 'gx'), may hold values from 0 to 31
- window_stop: int32 [4096, 128], P('ma', 'gx'), may hold values from 97 to 128
Outputs:
- solution: float32 [4096, 128, 128], P('ma', 'gx')
- residual: float32 [4096, 128, 128], P('ma', 'gx')
- direction: float32 [4096, 128, 128], P('ma', 'gx')
All inputs are finite; a program needn't handle non-finite values.
Results may differ from a plain program's by a relative error of at most 0.015.
Values may be sent and summed in bfloat16 or wider, within the bound.
A program may use at most 128 MiB of HBM per device.

v0:
```python
import math

import jax
import jax.numpy as jnp
from jax import lax
from jax.sharding import PartitionSpec as P

RAMP = 8


epsilon = 1e-06


def phase_table(freq_bins, length):
    samples = jnp.arange(length, dtype=jnp.int32)
    angles = (freq_bins[:, None] * samples[None, :] % length).astype(jnp.float32) * (
        2.0 * math.pi / length
    )
    return jnp.stack([jnp.cos(angles), -jnp.sin(angles)]) * math.sqrt(2.0 / length)


def taper_weights(window_start, window_stop, length):
    samples = jnp.arange(length, dtype=jnp.float32)
    rising = jnp.clip(
        (samples[None, None, :] - window_start[:, :, None].astype(jnp.float32) + 1.0) / RAMP,
        0.0,
        1.0,
    )
    falling = jnp.clip(
        (window_stop[:, :, None].astype(jnp.float32) - samples[None, None, :]) / RAMP, 0.0, 1.0
    )
    return rising * falling


def forward_transform(traces, table):
    return jnp.einsum("ast,cft->facs", traces, table, precision=lax.Precision.HIGHEST).astype(
        jnp.bfloat16
    )


def inverse_transform(spectra, table):
    return jnp.einsum(
        "facs,cft->ast", spectra.astype(jnp.float32), table, precision=lax.Precision.HIGHEST
    )


def forward_apply(model_traces, flat_kernel, table, weights):
    spectra = forward_transform(model_traces, table)
    arrived = lax.all_to_all(spectra, "gx", split_axis=0, concat_axis=3, tiled=True)
    half_rows = flat_kernel.shape[0] // 2
    sources = arrived.shape[3]
    incoming = lax.all_gather(arrived, "ma", axis=1, tiled=True)
    row_count = incoming.shape[1]
    product = jnp.dot(
        flat_kernel, incoming[0].reshape(row_count, 2 * sources), preferred_element_type=jnp.float32
    )
    upper_rows = product[:half_rows]
    lower_rows = product[half_rows:]
    real_part = upper_rows[:, :sources] - lower_rows[:, sources:]
    imaginary = upper_rows[:, sources:] + lower_rows[:, :sources]
    outgoing = jnp.stack([real_part, imaginary], 1).astype(jnp.bfloat16)[None]
    returned = lax.all_to_all(outgoing, "gx", split_axis=3, concat_axis=0, tiled=True)
    return weights * inverse_transform(returned, table)


def adjoint_apply(data_traces, flat_kernel, table, weights):
    spectra = forward_transform(weights * data_traces, table)
    arrived = lax.all_to_all(spectra, "gx", split_axis=0, concat_axis=3, tiled=True)
    sources = arrived.shape[3]
    real_part = arrived[0, :, 0, :]
    imaginary = arrived[0, :, 1, :]
    stacked = jnp.concatenate(
        [jnp.concatenate([real_part, imaginary], 1), jnp.concatenate([imaginary, -real_part], 1)], 0
    )
    summed = lax.psum_scatter(
        lax.dot_general(
            flat_kernel, stacked, (((0,), (0,)), ((), ())), preferred_element_type=jnp.float32
        ).astype(jnp.bfloat16),
        "ma",
        scatter_dimension=0,
        tiled=True,
    ).astype(jnp.float32)
    outgoing = summed.astype(jnp.bfloat16).reshape(summed.shape[0], 2, sources)[None]
    returned = lax.all_to_all(outgoing, "gx", split_axis=3, concat_axis=0, tiled=True)
    return inverse_transform(returned, table)


def per_device(recorded, kernel, freq_bins, window_start, window_stop):
    length = recorded.shape[2]
    table = phase_table(freq_bins, length)
    weights = taper_weights(window_start, window_stop, length)
    flat_kernel = kernel.reshape(2 * kernel.shape[2], kernel.shape[3])
    gradient = adjoint_apply(recorded, flat_kernel, table, weights)
    norm_start = lax.psum(jnp.sum(gradient * gradient), ("gx", "ma"))
    data_image = forward_apply(gradient, flat_kernel, table, weights)
    norm_data = lax.psum(jnp.sum(data_image * data_image), ("gx", "ma"))
    step_size = norm_start / (norm_data + epsilon)
    solution = step_size * gradient
    residual = recorded - step_size * data_image
    gradient_new = adjoint_apply(residual, flat_kernel, table, weights)
    norm_final = lax.psum(jnp.sum(gradient_new * gradient_new), ("gx", "ma"))
    direction = gradient_new + norm_final / (norm_start + epsilon) * gradient
    return (solution, residual, direction)


def solution(mesh):
    in_specs = (P("ma", "gx", None), P(None, "gx", "ma", None), P(), P("ma", "gx"), P("ma", "gx"))
    out_specs = (P("ma", "gx", None), P("ma", "gx", None), P("ma", "gx", None))
    return jax.shard_map(
        per_device, mesh=mesh, in_specs=in_specs, out_specs=out_specs, check_vma=False
    )
```

profile of v0, /device:TPU:0, one launch (start us, length us, event | category | flops | bytes accessed | tf_op | source)
XLA Modules:
  0.0 414.7 jit_solution(3050130807985677291)
XLA Ops:
  9.7 13.4 %fusion.38 = bf16[8,1024,2,16]{1,0,3,2:T(8,128)(2,1)S(1)} fusion(f32[1024,16,128]{2,1,0:T(8,128)} %param.5, f32[1024,16]{0,1:T(8,128)S(1)} %convert_element_type.69, f32[1024,16]{0,1:T(8,128)S(1)} %convert_element_type.68, f32[1,8,128]{2,1,0:T(8,128)S(1)} %get-tuple-element.26, f32[1,8,128]{2,1,0:T(8,128)S(1)} %get-tuple-element.25), kind=kOutput, calls=%fused_computation.40 | convolution fusion | flops 421793792 | bytes 9052160 | tf_op jit(solution)/shard_map/ast,cft->facs/dot_general | solution.py:36
  23.4 21.6 %all_to_all.108 = bf16[8,1024,2,16]{1,3,2,0:T(8,128)(2,1)S(1)} all-to-all(bf16[8,1024,2,16]{1,3,2,0:T(8,128)(2,1)S(1)} %copy.58), channel_id=1, replica_groups=mesh['gx'=8,'ma'=4] {'gx'}, dimensions={0} | all-to-all | bytes 1048576 | tf_op jit(solution)/shard_map/all_to_all | solution.py:68
  45.2 5.7 %fusion.11 = bf16[4096,256]{0,1:T(8,128)(2,1)} fusion(bf16[2048,4096]{1,0:T(8,128)(2,1)S(1)} %bitcast.154, bf16[1024,128]{0,1:T(8,128)(2,1)S(1)} %fusion.89, bf16[1024,128]{0,1:T(8,128)(2,1)S(1)} %get-tuple-element.24, bf16[1024,128]{0,1:T(8,128)(2,1)S(1)} %get-tuple-element.23), kind=kOutput, calls=%fused_computation.22 | convolution fusion | flops 4300210176 | bytes 19660800 | tf_op jit(solution)/shard_map/dot_general | solution.py:76
  50.9 30.3 %reduce-scatter.3.cloned.1.call-done = bf16[1024,256]{0,1:T(8,128)(2,1)} async-done(((bf16[4096,256]{0,1:T(8,128)(2,1)}), bf16[1024,256]{0,1:T(8,128)(2,1)}) %reduce-scatter.3.cloned.1.call-update) | async-done | bytes 524304 | tf_op jit(solution)/shard_map/reduce_scatter | solution.py:75
  82.8 20.1 %all_to_all.109 = bf16[1,1024,2,128]{1,2,0,3:T(2,128)(2,1)S(1)} all-to-all(bf16[1,1024,2,128]{1,2,0,3:T(2,128)(2,1)S(1)} %copy.63), channel_id=1, replica_groups=mesh['gx'=8,'ma'=4] {'gx'}, dimensions={3} | all-to-all | bytes 1048576 | tf_op jit(solution)/shard_map/all_to_all | solution.py:84
  111.4 6.9 %fusion.32 = bf16[8,1024,2,16]{1,0,3,2:T(8,128)(2,1)S(1)} fusion(f32[1024,16,128,1]{2,0,3,1:T(8,128)S(1)} %get-tuple-element.28, f32[1,8,128]{2,1,0:T(8,128)S(1)} %get-tuple-element.26, f32[1,8,128]{2,1,0:T(8,128)S(1)} %get-tuple-element.25), kind=kOutput, calls=%fused_computation.38 | convolution fusion | flops 402919424 | bytes 8921088 | tf_op jit(solution)/shard_map/ast,cft->facs/dot_general | solution.py:36
  118.6 17.5 %all_to_all.110 = bf16[8,1024,2,16]{1,3,2,0:T(8,128)(2,1)S(1)} all-to-all(bf16[8,1024,2,16]{1,3,2,0:T(8,128)(2,1)S(1)} %copy.66), channel_id=1, replica_groups=mesh['gx'=8,'ma'=4] {'gx'}, dimensions={0} | all-to-all | bytes 1048576 | tf_op jit(solution)/shard_map/all_to_all | solution.py:49
  137.2 20.6 %all-gather.2.cloned.1.call-done = bf16[1,4096,2,128]{1,3,2,0:T(8,128)(2,1)} async-done(((bf16[1,1024,2,128]{1,3,2,0:T(8,128)(2,1)}), bf16[1,4096,2,128]{1,3,2,0:T(8,128)(2,1)}) %all-gather.2.cloned.1.call-update) | async-done | bytes 2097168 | tf_op jit(solution)/shard_map/all_gather | solution.py:52
  157.8 8.7 %convolution_bitcast_fusion = f32[2048,256]{0,1:T(8,128)S(1)} fusion(bf16[4096,256]{0,1:T(8,128)(2,1)} %bitcast.158, bf16[2048,4096]{1,0:T(8,128)(2,1)} %bitcast.153), kind=kOutput, calls=%fused_computation.34 | convolution fusion | flops 4294967296 | bytes 20971520 | tf_op jit(solution)/shard_map/dot_general | solution.py:54
  167.3 20.2 %all_to_all.111 = bf16[1,1024,2,128]{1,2,0,3:T(2,128)(2,1)S(1)} all-to-all(bf16[1,1024,2,128]{1,2,0,3:T(2,128)(2,1)S(1)} %copy.68), channel_id=1, replica_groups=mesh['gx'=8,'ma'=4] {'gx'}, dimensions={3} | all-to-all | bytes 1048576 | tf_op jit(solution)/shard_map/all_to_all | solution.py:62
  187.5 11.4 %multiply_reduce_fusion = (f32[]{:T(128)}, f32[1024,16,128,1]{2,0,3,1:T(8,128)}) fusion(f32[1024,16]{0,1:T(8,128)S(1)} %convert_element_type.69, f32[1024,16]{0,1:T(8,128)S(1)} %convert_element_type.68, f32[1,8,128]{2,1,0:T(8,128)S(1)} %get-tuple-element.26, f32[1,8,128]{2,1,0:T(8,128)S(1)} %get-tuple-element.25, bf16[1,1024,2,8,16]{1,2,4,3,0:T(2,128)(2,1)S(1)} %bitcast.152), kind=kOutput, calls=%fused_computation.16 | convolution fusion | flops 425725952 | bytes 9052164 | tf_op jit(solution)/shard_map/facs,cft->ast/dot_general | solution.py:42
  199.0 39.0 %all-reduce = (f32[]{:T(128)}, f32[]{:T(128)}) all-reduce(f32[]{:T(128)} %get-tuple-element.27, f32[]{:T(128)} %get-tuple-element.29), channel_id=1, replica_groups=mesh['gx'=8,'ma'=4] {'gx','ma'}, use_global_device_ids=true, to_apply=%region_2.3 | all-reduce | flops 2 | bytes 16 | tf_op jit(solution)/shard_map/psum | solution.py:94
  239.3 9.3 %multiply_subtract_fusion = f32[1024,16,128]{2,0,1:T(8,128)S(1)} fusion(f32[1024,16,128]{2,1,0:T(8,128)} %param.5, f32[]{:T(128)S(6)} %div.14, f32[1024,16,128,1]{2,0,3,1:T(8,128)} %get-tuple-element.30, f32[1024,16]{0,1:T(8,128)S(1)} %convert_element_type.69, f32[1024,16]{0,1:T(8,128)S(1)} %convert_element_type.68), kind=kLoop, calls=%fused_computation.15 | loop fusion | flops 23068672 | bytes 25296900 | tf_op jit(solution)/shard_map/sub | solution.py:99
  248.6 13.1 %fusion.35 = bf16[8,1024,2,16]{1,0,3,2:T(8,128)(2,1)S(1)} fusion(f32[1024,16,128]{2,0,1:T(8,128)S(1)} %multiply_subtract_fusion, f32[1024,16]{0,1:T(8,128)S(1)} %convert_element_type.69, f32[1024,16]{0,1:T(8,128)S(1)} %convert_element_type.68, f32[1,8,128]{2,1,0:T(8,128)S(1)} %get-tuple-element.26, f32[1,8,128]{2,1,0:T(8,128)S(1)} %get-tuple-element.25), kind=kOutput, calls=%fused_computation.39 | convolution fusion | flops 421793792 | bytes 9052160 | tf_op jit(solution)/shard_map/ast,cft->facs/dot_general | solution.py:36
  262.0 17.7 %all_to_all.112 = bf16[8,1024,2,16]{1,3,2,0:T(8,128)(2,1)S(1)} all-to-all(bf16[8,1024,2,16]{1,3,2,0:T(8,128)(2,1)S(1)} %copy.72), channel_id=1, replica_groups=mesh['gx'=8,'ma'=4] {'gx'}, dimensions={0} | all-to-all | bytes 1048576 | tf_op jit(solution)/shard_map/all_to_all | solution.py:68
  279.9 5.7 %fusion.12 = bf16[4096,256]{0,1:T(8,128)(2,1)} fusion(bf16[2048,4096]{1,0:T(8,128)(2,1)S(1)} %bitcast.157, bf16[1024,128]{0,1:T(8,128)(2,1)S(1)} %fusion.90, bf16[1024,128]{0,1:T(8,128)(2,1)S(1)} %get-tuple-element.22, bf16[1024,128]{0,1:T(8,128)(2,1)S(1)} %get-tuple-element.21), kind=kOutput, calls=%fused_computation.23 | convolution fusion | flops 4300210176 | bytes 19660800 | tf_op jit(solution)/shard_map/dot_general | solution.py:76
  285.6 30.0 %reduce-scatter.5.cloned.1.call-done = bf16[1024,256]{0,1:T(8,128)(2,1)} async-done(((bf16[4096,256]{0,1:T(8,128)(2,1)}), bf16[1024,256]{0,1:T(8,128)(2,1)}) %reduce-scatter.5.cloned.1.call-update) | async-done | bytes 524304 | tf_op jit(solution)/shard_map/reduce_scatter | solution.py:75
  318.0 5.7 %all-to-all-start.5 = ((bf16[1,1024,2,128]{1,2,0,3:T(2,128)(2,1)}), bf16[1,1024,2,128]{1,2,0,3:T(2,128)(2,1)S(1)}, u32[]{:S(2)}, u32[]{:S(2)}) async-start(bf16[1,1024,2,128]{1,2,0,3:T(2,128)(2,1)} %copy.77), calls=%async_computation.7 | async-start | bytes 1048576 | tf_op jit(solution)/shard_map/all_to_all | solution.py:84
  324.3 11.6 %copy.81 = f32[1024,16,128]{2,1,0:T(8,128)} copy(f32[1024,16,128]{2,0,1:T(8,128)} %copy-done.1) | data formatting | bytes 16777216
  338.0 7.2 %fusion = (f32[]{:T(128)}, f32[1024,16,128,1]{2,0,3,1:T(8,128)}) fusion(f32[1,8,128]{2,1,0:T(8,128)S(1)} %get-tuple-element.26, f32[1,8,128]{2,1,0:T(8,128)S(1)} %get-tuple-element.25, bf16[1,1024,2,8,16]{1,2,4,3,0:T(2,128)(2,1)S(1)} %bitcast.148), kind=kOutput, calls=%fused_computation.2 | convolution fusion | flops 406851584 | bytes 8921092 | tf_op jit(solution)/shard_map/facs,cft->ast/dot_general | solution.py:42
  345.2 38.8 %psum.23 = f32[]{:T(128)} all-reduce(f32[]{:T(128)} %get-tuple-element.31), channel_id=1, replica_groups=mesh['gx'=8,'ma'=4] {'gx','ma'}, use_global_device_ids=true, to_apply=%region_7.8 | all-reduce | flops 1 | bytes 8 | tf_op jit(solution)/shard_map/psum | solution.py:101
  384.7 6.7 %bitcast_add_fusion = (f32[1024,16,128]{2,0,1:T(8,128)S(1)}, f32[1024,16,128]{2,0,1:T(8,128)S(1)}) fusion(f32[1024,16,128,1]{2,0,3,1:T(8,128)} %get-tuple-element.32, f32[1024,16,128,1]{2,0,3,1:T(8,128)} %copy-done, f32[]{:T(128)S(6)} %div.15, f32[]{:T(128)S(6)} %div.14), kind=kLoop, calls=%fused_computation | loop fusion | flops 6291456 | bytes 33554440 | tf_op jit(solution)/shard_map/add | solution.py:102
  391.4 8.3 %copy.82 = f32[1024,16,128]{2,1,0:T(8,128)} copy(f32[1024,16,128]{2,0,1:T(8,128)S(1)} %get-tuple-element.17) | data formatting | bytes 16777216
  399.6 8.3 %copy.80 = f32[1024,16,128]{2,1,0:T(8,128)} copy(f32[1024,16,128]{2,0,1:T(8,128)S(1)} %get-tuple-element.18) | data formatting | bytes 16777216
  (41 shorter events, 20.0 us)
Async XLA Ops:
  7.2 74.0 %reduce-scatter.3.cloned.1.call-start = ((), (), s32[]{:S(2)}) async-start(), calls=%async_computation.8 | async-start | bytes 2621440 | tf_op jit(solution)/shard_map/reduce_scatter | solution.py:75
  9.7 35.5 %copy-start.2 = (bf16[2,1,1024,4096]{3,2,1,0:T(8,128)(2,1)S(1)}, bf16[2,1,1024,4096]{3,2,1,0:T(8,128)(2,1)}, u32[]{:S(2)}) copy-start(bf16[2,1,1024,4096]{3,2,1,0:T(8,128)(2,1)} %param.6) | copy-start | bytes 50331652
  50.9 107.0 %all-gather.2.cloned.1.call-start = ((), (), s32[]{:S(2)}) async-start(), calls=%async_computation.9 | async-start | bytes 2621440 | tf_op jit(solution)/shard_map/all_gather | solution.py:52
  108.0 3.4 copy-start
  137.0 178.6 %reduce-scatter.5.cloned.1.call-start = ((), (), s32[]{:S(2)}) async-start(), calls=%async_computation.10 | async-start | bytes 2621440 | tf_op jit(solution)/shard_map/reduce_scatter | solution.py:75
  239.2 40.6 %slice-start = ((s8[16777216]{0:T(1024)(128)(4,1)}), s8[4194304]{0:T(1024)(128)(4,1)S(1)}, s32[]{:S(2)}) async-start(s8[16777216]{0:T(1024)(128)(4,1)} %bitcast.155), calls=%async_computation.11 | async-start | bytes 8388608
  239.2 40.6 %slice-start.1 = ((s8[16777216]{0:T(1024)(128)(4,1)}), s8[4194304]{0:T(1024)(128)(4,1)S(1)}, s32[]{:S(2)}) async-start(s8[16777216]{0:T(1024)(128)(4,1)} %bitcast.155), calls=%async_computation.12 | async-start | bytes 8388608
  239.3 40.6 %slice-start.2 = ((s8[16777216]{0:T(1024)(128)(4,1)}), s8[4194304]{0:T(1024)(128)(4,1)S(1)}, s32[]{:S(2)}) async-start(s8[16777216]{0:T(1024)(128)(4,1)} %bitcast.155), calls=%async_computation.13 | async-start | bytes 8388608
  248.6 13.1 %copy-start.1 = (f32[1024,16,128]{2,0,1:T(8,128)}, f32[1024,16,128]{2,0,1:T(8,128)S(1)}, u32[]{:S(2)}) copy-start(f32[1024,16,128]{2,0,1:T(8,128)S(1)} %multiply_subtract_fusion) | copy-start | bytes 25165828
  248.6 31.3 %slice-start.3 = ((s8[16777216]{0:T(1024)(128)(4,1)}), s8[4194304]{0:T(1024)(128)(4,1)S(1)}, s32[]{:S(2)}) async-start(s8[16777216]{0:T(1024)(128)(4,1)} %bitcast.155), calls=%async_computation.14 | async-start | bytes 8388608
  318.0 20.0 %all-to-all-start.5 = ((bf16[1,1024,2,128]{1,2,0,3:T(2,128)(2,1)}), bf16[1,1024,2,128]{1,2,0,3:T(2,128)(2,1)S(1)}, u32[]{:S(2)}, u32[]{:S(2)}) async-start(bf16[1,1024,2,128]{1,2,0,3:T(2,128)(2,1)} %copy.77), calls=%async_computation.7 | async-start | bytes 1048576 | tf_op jit(solution)/shard_map/all_to_all | solution.py:84
Sparse Core Ops, SparseCore 0:
  51.0 30.1 reduce-scatter.2
  137.1 20.6 all-gather.1
  285.7 29.8 reduce-scatter.4
where the time goes:
time: 419 us; the launch traced here: 415 us
  blocking collectives  175 us (42%)
  waiting for transfers between devices  83 us (20%)
  matrix products  77.3 us (18%)
  local copies, waits for them, and re-layouts  37.9 us (9%)
  other arithmetic  18.7 us (4%)
  between operations  16.8 us (4%)
  starting transfers between devices  6.02 us (1%)
    reduce_scatter x2, waiting for transfers between devices, adjoint_apply(): lax.psum_scatter(lax.dot_general(flat_kernel, stacked, (((0,), (0,)), (()...  60.3 us
    all_to_all x2, blocking collectives, adjoint_apply(): lax.all_to_all(spectra, 'gx', split_axis=0, concat_axis=3, tiled=True)  39.3 us
    psum x1, blocking collectives, per_device(): norm_start = lax.psum(jnp.sum(gradient * gradient), ('gx', 'ma'))  39 us
    psum x1, blocking collectives, per_device(): norm_final = lax.psum(jnp.sum(gradient_new * gradient_new), ('gx', 'ma'))  38.8 us
    dot_general x3, matrix products, forward_transform(): jnp.einsum('ast,cft->facs', traces, table, precision=lax.Precision.HIGHEST)  33.4 us
    unnamed x17, local copies, waits for them, and re-layouts  31.6 us
    dot_general x3, matrix products, inverse_transform(): jnp.einsum('facs,cft->ast', spectra.astype(jnp.float32), table, precision...  23.8 us
    all_gather x1, waiting for transfers between devices, forward_apply(): incoming = lax.all_gather(arrived, 'ma', axis=1, tiled=True)  20.6 us
  transfers between devices with their start and end apart: 4, of which 4 were waited for; matrix products, arithmetic and copies ran while one was open for 3% of the time, Pallas kernels for 0%

commit v1 on v0

v1 whole, which is shorter than its diff:
```python
import functools
import math

import jax
import jax.numpy as jnp
from jax import lax
from jax.experimental import pallas as pl
from jax.experimental.pallas import tpu as pltpu
from jax.sharding import PartitionSpec as P

RAMP = 8
MESH = pl.DeviceIdType.MESH

epsilon = 1e-06


def phase_table(freq_bins, length):
    samples = jnp.arange(length, dtype=jnp.int32)
    angles = (freq_bins[:, None] * samples[None, :] % length).astype(jnp.float32) * (
        2.0 * math.pi / length
    )
    return jnp.stack([jnp.cos(angles), -jnp.sin(angles)], 1) * math.sqrt(2.0 / length)


def taper_weights(window_start, window_stop, length):
    samples = jnp.arange(length, dtype=jnp.float32)
    rising = jnp.clip(
        (samples[None, None, :] - window_start[:, :, None].astype(jnp.float32) + 1.0) / RAMP,
        0.0,
        1.0,
    )
    falling = jnp.clip(
        (window_stop[:, :, None].astype(jnp.float32) - samples[None, None, :]) / RAMP, 0.0, 1.0
    )
    return rising * falling


def exchange_kernel(n, x_ref, o_ref, send_sem, recv_sem, own_sem):
    me = lax.axis_index("gx")
    barrier = pltpu.get_barrier_semaphore()
    for k in range(1, n):
        pl.semaphore_signal(
            barrier, inc=1, device_id={"gx": lax.rem(me + k, n)}, device_id_type=MESH
        )
    own = pltpu.make_async_copy(x_ref.at[me], o_ref.at[me], own_sem)
    own.start()
    pl.semaphore_wait(barrier, n - 1)
    copies = []
    for k in range(1, n):
        peer = lax.rem(me + k, n)
        copy = pltpu.make_async_remote_copy(
            src_ref=x_ref.at[peer],
            dst_ref=o_ref.at[me],
            send_sem=send_sem.at[k],
            recv_sem=recv_sem.at[k],
            device_id={"gx": peer},
            device_id_type=MESH,
        )
        copy.start()
        copies.append(copy)
    own.wait()
    for copy in copies:
        copy.wait()


def exchange(x, n, number):
    return pl.pallas_call(
        functools.partial(exchange_kernel, n),
        out_shape=jax.ShapeDtypeStruct(x.shape, x.dtype),
        in_specs=[pl.BlockSpec(memory_space=pltpu.VMEM)],
        out_specs=pl.BlockSpec(memory_space=pltpu.VMEM),
        scratch_shapes=[
            pltpu.SemaphoreType.DMA((n,)),
            pltpu.SemaphoreType.DMA((n,)),
            pltpu.SemaphoreType.DMA,
        ],
        compiler_params=pltpu.CompilerParams(collective_id=number, has_side_effects=True),
        name=f"exchange{number}",
    )(x)


def total_kernel(outer, inner, x_ref, o_ref, held, send_sem, recv_sem):
    n = outer * inner
    me = lax.axis_index("gx") * inner + lax.axis_index("ma")
    barrier = pltpu.get_barrier_semaphore()

    def place(k):
        peer = lax.rem(me + k, n)
        return (peer // inner, lax.rem(peer, inner))

    for k in range(1, n):
        pl.semaphore_signal(barrier, inc=1, device_id=place(k), device_id_type=MESH)
    pl.semaphore_wait(barrier, n - 1)
    copies = []
    for k in range(1, n):
        copy = pltpu.make_async_remote_copy(
            src_ref=x_ref,
            dst_ref=held.at[me],
            send_sem=send_sem.at[k],
            recv_sem=recv_sem.at[k],
            device_id=place(k),
            device_id_type=MESH,
        )
        copy.start()
        copies.append(copy)
    held[me] = x_ref[...]
    for copy in copies:
        copy.wait()
    o_ref[...] = jnp.sum(held[...], axis=0)


def total(x, outer, inner, number):
    n = outer * inner
    return pl.pallas_call(
        functools.partial(total_kernel, outer, inner),
        out_shape=jax.ShapeDtypeStruct(x.shape, x.dtype),
        in_specs=[pl.BlockSpec(memory_space=pltpu.VMEM)],
        out_specs=pl.BlockSpec(memory_space=pltpu.VMEM),
        scratch_shapes=[
            pltpu.VMEM((n,) + x.shape, x.dtype),
            pltpu.SemaphoreType.DMA((n,)),
            pltpu.SemaphoreType.DMA((n,)),
        ],
        compiler_params=pltpu.CompilerParams(collective_id=number, has_side_effects=True),
        name=f"total{number}",
    )(x)


def pairs(n, bit):
    return [(i, i ^ bit) for i in range(n)]


def scatter_sum(partial, n):
    rows, block = partial.shape[1:]
    me = lax.axis_index("ma")
    held = partial
    bit = 1
    while bit < n:
        own = (me // bit) % 2
        parts = held.reshape(-1, 2, rows, block)
        keep = lax.dynamic_index_in_dim(parts, own, 1, keepdims=False)
        send = lax.dynamic_index_in_dim(parts, 1 - own, 1, keepdims=False)
        got = lax.ppermute(send, "ma", pairs(n, bit))
        held = (keep.astype(jnp.float32) + got.astype(jnp.float32)).astype(jnp.bfloat16)
        bit *= 2
    return held.reshape(rows, block)


def gather_all(x, n):
    rows, block = x.shape
    me = lax.axis_index("ma")
    held = x.reshape(rows, 1, block)
    bit = n // 2
    while bit >= 1:
        own = (me // bit) % 2
        got = lax.ppermute(held, "ma", pairs(n, bit))
        first = jnp.where(own == 0, held, got)
        second = jnp.where(own == 0, got, held)
        held = jnp.stack([first, second], 2).reshape(rows, -1, block)
        bit //= 2
    return held.reshape(rows, n * block)


def to_spectra(traces, table):
    freqs = table.shape[0]
    flat = table.reshape(2 * freqs, table.shape[2]).astype(jnp.bfloat16)
    out = jnp.einsum(
        "ast,kt->ksa", traces.astype(jnp.bfloat16), flat, preferred_element_type=jnp.float32
    ).astype(jnp.bfloat16)
    return out.reshape(freqs, 2 * out.shape[1], out.shape[2])


def to_traces(spectra, table):
    freqs, double, points = spectra.shape
    sources = double // 2
    length = table.shape[2]
    depth = freqs * double
    across = spectra.reshape(depth, points).T
    owner = jnp.arange(depth, dtype=jnp.int32) % sources
    mask = (owner[None, :] == jnp.arange(sources, dtype=jnp.int32)[:, None]).astype(jnp.bfloat16)
    spread = (across[:, None, :] * mask[None]).reshape(points * sources, depth)
    tall = jnp.repeat(table.reshape(2 * freqs, length).astype(jnp.bfloat16), sources, axis=0)
    out = jnp.dot(spread, tall, preferred_element_type=jnp.float32)
    return out.reshape(points, sources, length)


def by_frequency(arrived, n):
    sources = arrived.shape[1] // 2
    points = arrived.shape[2]
    return arrived.reshape(n, 2, sources, points).transpose(1, 0, 2, 3).reshape(2, -1, points)


def by_source(spectra, n):
    points = spectra.shape[2]
    sources = spectra.shape[1] // n
    return spectra.reshape(2, n, sources, points).transpose(1, 0, 2, 3).reshape(n, -1, points)


def adjoint_kernel(d_ref, k_ref, o_ref):
    half = d_ref.shape[0] // 2
    data = d_ref[...]
    first = jnp.dot(data, k_ref[0], preferred_element_type=jnp.float32)
    second = jnp.dot(data, k_ref[1], preferred_element_type=jnp.float32)
    o_ref[0, :half] = (first[:half] + second[half:]).astype(o_ref.dtype)
    o_ref[0, half:] = (first[half:] - second[:half]).astype(o_ref.dtype)


def adjoint_product(data, flat_kernel, inner):
    sources, rows = data.shape[1], data.shape[2]
    columns = flat_kernel.shape[1]
    block = columns // inner
    tile = min(512, block)
    per_block = block // tile
    partial = pl.pallas_call(
        adjoint_kernel,
        grid=(columns // tile,),
        out_shape=jax.ShapeDtypeStruct((inner, 2 * sources, block), jnp.bfloat16),
        in_specs=[
            pl.BlockSpec((2 * sources, rows), lambda j: (0, 0)),
            pl.BlockSpec((2, rows, tile), lambda j: (0, 0, j)),
        ],
        out_specs=pl.BlockSpec(
            (1, 2 * sources, tile), lambda j: (j // per_block, 0, j % per_block)
        ),
        compiler_params=pltpu.CompilerParams(vmem_limit_bytes=60 * 1024 * 1024),
        cost_estimate=pl.CostEstimate(
            flops=8 * sources * rows * columns,
            bytes_accessed=4 * rows * columns + 4 * sources * (rows + columns),
            transcendentals=0,
        ),
        name="adjoint",
    )(data.reshape(2 * sources, rows), flat_kernel.reshape(2, rows, columns))
    return scatter_sum(partial, inner).reshape(2, sources, block)


def final_kernel(
    sums_ref, rec_ref, win_ref, g_ref, d_ref, h_ref, tall_ref, mask_ref, pick_ref,
    sol_ref, res_ref, dir_ref,
):
    tile, sources, length = rec_ref.shape
    norm_start, norm_data = sums_ref[0, 0], sums_ref[1, 0]
    cross, norm_change = sums_ref[2, 0], sums_ref[3, 0]
    step_size = norm_start / (norm_data + epsilon)
    norm_final = norm_start - 2.0 * step_size * cross + step_size * step_size * norm_change
    ratio = norm_final / (norm_start + epsilon)
    tall = tall_ref[...]

    def rows(values, mask):
        return (values[:, None, :] * mask[None]).reshape(tile * sources, -1).astype(jnp.bfloat16)

    def traces(ref):
        spread = rows(ref[...].astype(jnp.float32), mask_ref[...])
        out = jnp.dot(spread, tall, preferred_element_type=jnp.float32)
        return out.reshape(tile, sources, length)

    gradient = traces(g_ref)
    change = traces(h_ref)
    sol_ref[...] = step_size * gradient
    dir_ref[...] = (gradient - step_size * change) + ratio * gradient
    window = win_ref[...]
    ones = jnp.ones((window.shape[1], length), jnp.bfloat16)
    shape = (tile, sources, length)
    start = jnp.dot(rows(window, pick_ref[0]), ones, preferred_element_type=jnp.float32)
    stop = jnp.dot(rows(window, pick_ref[1]), ones, preferred_element_type=jnp.float32)
    samples = lax.broadcasted_iota(jnp.int32, shape, 2).astype(jnp.float32)
    rising = jnp.clip((samples - start.reshape(shape) + 1.0) / RAMP, 0.0, 1.0)
    falling = jnp.clip((stop.reshape(shape) - samples) / RAMP, 0.0, 1.0)
    image = (rising * falling) * traces(d_ref)
    res_ref[...] = rec_ref[...] - step_size * image


def final_step(sums, recorded, window_start, window_stop, returned, arrived, changed, table):
    points, sources, length = recorded.shape
    depth = returned.shape[0] * returned.shape[1]
    tile = min(128, points)

    def across(x):
        return x.reshape(depth, points).T

    place = jnp.arange(sources, dtype=jnp.int32)
    owner = jnp.arange(depth, dtype=jnp.int32) % sources
    mask = (owner[None, :] == place[:, None]).astype(jnp.float32)
    column = jnp.arange(2 * sources, dtype=jnp.int32)
    pick = jnp.stack(
        [column[None, :] == place[:, None], column[None, :] == place[:, None] + sources]
    ).astype(jnp.float32)
    tall = jnp.repeat(table.reshape(-1, length).astype(jnp.bfloat16), sources, axis=0)
    window = jnp.concatenate([window_start, window_stop], 1).astype(jnp.float32)
    whole3 = pl.BlockSpec((tile, sources, length), lambda i: (i, 0, 0))
    strip = pl.BlockSpec((tile, depth), lambda i: (i, 0))
    return pl.pallas_call(
        final_kernel,
        grid=(points // tile,),
        out_shape=[jax.ShapeDtypeStruct(recorded.shape, jnp.float32)] * 3,
        in_specs=[
            pl.BlockSpec(memory_space=pltpu.SMEM),
            whole3,
            pl.BlockSpec((tile, 2 * sources), lambda i: (i, 0)),
            strip,
            strip,
            strip,
            pl.BlockSpec((depth, length), lambda i: (0, 0)),
            pl.BlockSpec((sources, depth), lambda i: (0, 0)),
            pl.BlockSpec((2, sources, 2 * sources), lambda i: (0, 0, 0)),
        ],
        out_specs=[whole3] * 3,
        compiler_params=pltpu.CompilerParams(vmem_limit_bytes=48 * 1024 * 1024),
        cost_estimate=pl.CostEstimate(
            flops=8 * points * sources * depth * length,
            bytes_accessed=16 * points * sources * length,
            transcendentals=0,
        ),
        name="final",
    )(sums, recorded, window, across(returned), across(arrived), across(changed), tall, mask, pick)


def forward_product(model, flat_kernel, inner):
    sources = model.shape[1]
    incoming = gather_all(model.reshape(2 * sources, -1), inner)
    product = lax.dot_general(
        incoming, flat_kernel, (((1,), (1,)), ((), ())), preferred_element_type=jnp.float32
    )
    half = flat_kernel.shape[0] // 2
    real_part = product[:sources, :half] - product[sources:, half:]
    imaginary = product[sources:, :half] + product[:sources, half:]
    return jnp.stack([real_part, imaginary], 0).astype(jnp.bfloat16)


def per_device(outer, inner, recorded, kernel, freq_bins, window_start, window_stop):
    length = recorded.shape[2]
    table = phase_table(freq_bins, length)
    weights = taper_weights(window_start, window_stop, length)
    flat_kernel = kernel.reshape(2 * kernel.shape[2], kernel.shape[3])

    data = by_frequency(exchange(to_spectra(weights * recorded, table), outer, 0), outer)
    adjoint = adjoint_product(data, flat_kernel, inner)
    returned = lax.all_to_all(
        by_source(adjoint, outer), "gx", split_axis=0, concat_axis=0, tiled=True
    )

    same = freq_bins[:, None] == freq_bins[None, :]
    repeated = jnp.sum(same.astype(jnp.int32)) > freq_bins.shape[0]

    def combined(spectra):
        parts = lax.all_to_all(
            by_source(spectra, outer), "gx", split_axis=0, concat_axis=0, tiled=True
        )
        mixed = jnp.einsum(
            "gf,fxa->gxa",
            same.astype(jnp.bfloat16),
            parts,
            preferred_element_type=jnp.float32,
        ).astype(jnp.bfloat16)
        back = lax.all_to_all(mixed, "gx", split_axis=0, concat_axis=0, tiled=True)
        return by_frequency(back, outer)

    model = lax.cond(repeated, combined, lambda spectra: spectra, adjoint)
    outgoing = by_source(forward_product(model, flat_kernel, inner), outer)
    imaged = exchange(outgoing, outer, 1)
    image = weights * to_traces(imaged, table)
    second = by_frequency(exchange(to_spectra(weights * image, table), outer, 2), outer)
    normal = adjoint_product(second, flat_kernel, inner)
    changed = exchange(by_source(normal, outer), outer, 3)

    double, points = returned.shape[1:]
    depth = freq_bins.shape[0] * double
    eye = jnp.eye(double, dtype=jnp.bfloat16)
    mixing = (same.astype(jnp.bfloat16)[:, None, :, None] * eye[None, :, None, :]).reshape(
        depth, depth
    )
    flat_g = returned.reshape(depth, points)
    flat_h = changed.reshape(depth, points)
    mixed_g = jnp.dot(mixing, flat_g, preferred_element_type=jnp.float32)
    mixed_h = jnp.dot(mixing, flat_h, preferred_element_type=jnp.float32)
    sums = jnp.stack(
        [
            jnp.sum(flat_g.astype(jnp.float32) * mixed_g),
            jnp.sum(image * image),
            jnp.sum(mixed_g * flat_h.astype(jnp.float32)),
            jnp.sum(flat_h.astype(jnp.float32) * mixed_h),
        ]
    )
    sums = total(jnp.broadcast_to(jnp.tile(sums, 2)[:, None], (8, 128)), outer, inner, 4)
    if recorded.shape[1] % 8 == 0:
        return tuple(
            final_step(
                sums, recorded, window_start, window_stop, returned, imaged, changed, table
            )
        )
    gradient = to_traces(returned, table)
    change = to_traces(changed, table)
    norm_start, norm_data, cross, norm_change = sums[0, 0], sums[1, 0], sums[2, 0], sums[3, 0]
    step_size = norm_start / (norm_data + epsilon)
    norm_final = norm_start - 2.0 * step_size * cross + step_size * step_size * norm_change
    solution = step_size * gradient
    residual = recorded - step_size * image
    direction = gradient - step_size * change + norm_final / (norm_start + epsilon) * gradient
    return (solution, residual, direction)


def solution(mesh):
    in_specs = (P("ma", "gx", None), P(None, "gx", "ma", None), P(), P("ma", "gx"), P("ma", "gx"))
    out_specs = (P("ma", "gx", None), P("ma", "gx", None), P("ma", "gx", None))
    return jax.shard_map(
        functools.partial(per_device, mesh.shape["gx"], mesh.shape["ma"]),
        mesh=mesh,
        in_specs=in_specs,
        out_specs=out_specs,
        check_vma=False,
    )
```

time: 419 us -> 239 us (0.57)
  blocking collectives: 175 us -> 0 us
  Pallas kernels: 0 us -> 117 us
  matrix products: 77.3 us -> 33.4 us
  waiting for transfers between devices: 83 us -> 40 us
  local copies, waits for them, and re-layouts: 37.9 us -> 18.4 us
  between operations: 16.8 us -> 1.59 us
  starting transfers between devices: 6.02 us -> 12.4 us
  other arithmetic: 18.7 us -> 13.6 us
    pallas_call x0 -> x8, Pallas kernels: none -> 117 us  [the longest x4 65.6 us: exchange(): pl.pallas_call(functools.partial(exchange_kernel, n), out_shape=jax.Shape...]
    all_to_all x5 -> x0, blocking collectives: 97.2 us -> none  [the longest x2 39.3 us: adjoint_apply(): lax.all_to_all(spectra, 'gx', split_axis=0, concat_axis=3, tiled=True)]
    psum x2 -> x0, blocking collectives: 77.8 us -> none  [the longest x1 39 us: per_device(): norm_start = lax.psum(jnp.sum(gradient * gradient), ('gx', 'ma'))]
    reduce_scatter x2 -> x0, waiting for transfers between devices: 60.3 us -> none  [adjoint_apply(): lax.psum_scatter(lax.dot_general(flat_kernel, stacked, (((0,), (0,)), (()...]
    dot_general x9 -> x6, matrix products: 77.3 us -> 33.4 us  [the longest x2 14.9 us: to_spectra(): jnp.einsum('ast,kt->ksa', traces.astype(jnp.bfloat16), flat, preferred_el...]
    unnamed x17 -> x8, local copies, waits for them, and re-layouts: 31.6 us -> 0.69 us
    ppermute x0 -> x6, waiting for transfers between devices: none -> 29.9 us  [the longest x4 15.4 us: scatter_sum(): got = lax.ppermute(send, 'ma', pairs(n, bit))]
    all_gather x1 -> x0, waiting for transfers between devices: 20.6 us -> none  [forward_apply(): incoming = lax.all_gather(arrived, 'ma', axis=1, tiled=True)]
  transfers between devices with their start and end apart: 4 -> 7, of which waited for: 4 -> 6; matrix products, arithmetic and copies ran while one was open for 3% -> 2% of each run, Pallas kernels for 0% -> 0%
where the time goes in v1:
time: 239 us; the launch traced here: 237 us
  Pallas kernels  117 us (49%)
  waiting for transfers between devices  40 us (17%)
  matrix products  33.4 us (14%)
  local copies, waits for them, and re-layouts  18.4 us (8%)
  other arithmetic  13.6 us (6%)
  starting transfers between devices  12.4 us (5%)
    pallas_call x4, Pallas kernels, exchange(): pl.pallas_call(functools.partial(exchange_kernel, n), out_shape=jax.Shape...  65.6 us
    pallas_call x2, Pallas kernels, adjoint_product(): pl.pallas_call(adjoint_kernel, grid=(columns // tile,), out_shape=jax.Sha...  23.1 us
    pallas_call x1, Pallas kernels, final_step(): pl.pallas_call(final_kernel, grid=(points // tile,), out_shape=[jax.Shape...  15.7 us
    ppermute x4, waiting for transfers between devices, scatter_sum(): got = lax.ppermute(send, 'ma', pairs(n, bit))  15.4 us
    dot_general x2, matrix products, to_spectra(): jnp.einsum('ast,kt->ksa', traces.astype(jnp.bfloat16), flat, preferred_el...  14.9 us
    ppermute x2, waiting for transfers between devices, gather_all(): got = lax.ppermute(held, 'ma', pairs(n, bit))  14.4 us
    pallas_call x1, Pallas kernels, total(): pl.pallas_call(functools.partial(total_kernel, outer, inner), out_shape=j...  13 us
    all_to_all x1, waiting for transfers between devices, per_device(): lax.all_to_all(by_source(adjoint, outer), 'gx', split_axis=0, concat_axis...  10.1 us
  transfers between devices with their start and end apart: 7, of which 6 were waited for; matrix products, arithmetic and copies ran while one was open for 2% of the time, Pallas kernels for 0%

profile of v1, /device:TPU:0, one launch (start us, length us, event | category | flops | bytes accessed | tf_op | source)
XLA Modules:
  0.0 237.0 jit_solution(6633918178760804108)
XLA Ops:
  3.1 7.4 %fusion.18 = bf16[16,16,1024]{2,0,1:T(8,128)(2,1)S(1)} fusion(bf16[16,128,1]{1,0,2:T(8,128)(2,1)S(1)} %bitcast.141, f32[1024,16,128]{2,1,0:T(8,128)} %rec_ref.1, f32[1024,16]{0,1:T(8,128)S(1)} %convert_element_type.149, f32[1024,16]{0,1:T(8,128)S(1)} %convert_element_type.148), kind=kOutput, calls=%fused_computation.24 | convolution fusion | flops 88342528 | bytes 9048064 | tf_op jit(solution)/shard_map/ast,kt->ksa/dot_general | solution.py:167
  11.6 16.4 %exchange0.1 = bf16[8,32,1024]{2,1,0:T(8,128)(2,1)} custom-call(bf16[8,32,1024]{2,1,0:T(8,128)(2,1)} %bitcast.131), custom_call_target="tpu_custom_call" | custom-call | tf_op jit(solution)/shard_map/exchange0/pallas_call | solution.py:67
  28.0 1.9 copy.133
  29.9 11.6 %adjoint.2 = bf16[4,256,1024]{2,1,0:T(8,128)(2,1)} custom-call(bf16[256,1024]{1,0:T(8,128)(2,1)} %bitcast.121, bf16[2,1024,4096]{2,1,0:T(8,128)(2,1)} %bitcast.111), custom_call_target="tpu_custom_call" | custom-call | flops 4294967296 | bytes 19398656 | tf_op jit(solution)/shard_map/adjoint/pallas_call | solution.py:214
  42.9 2.6 %collective-permute-done = bf16[2,256,1024]{2,1,0:T(8,128)(2,1)S(1)} collective-permute-done((bf16[2,256,1024]{2,1,0:T(8,128)(2,1)S(1)}, bf16[2,256,1024]{2,1,0:T(8,128)(2,1)S(1)}, u32[]{:S(2)}, u32[]{:S(2)}) %collective-permute-start) | collective-permute-done | bytes 1048608 | tf_op jit(solution)/shard_map/ppermute | solution.py:143
  50.2 11.0 %collective-permute-done.1 = bf16[1,256,1024]{2,1,0:T(8,128)(2,1)S(1)} collective-permute-done((bf16[1,256,1024]{2,1,0:T(8,128)(2,1)S(1)}, bf16[1,256,1024]{2,1,0:T(8,128)(2,1)S(1)}, u32[]{:S(2)}, u32[]{:S(2)}) %collective-permute-start.1) | collective-permute-done | bytes 524320 | tf_op jit(solution)/shard_map/ppermute | solution.py:143
  63.3 11.6 %collective-permute-done.2 = bf16[256,1,1024]{2,0,1:T(8,128)(2,1)S(1)} collective-permute-done((bf16[256,1,1024]{2,0,1:T(8,128)(2,1)S(1)}, bf16[256,1,1024]{2,0,1:T(8,128)(2,1)S(1)}, u32[]{:S(2)}, u32[]{:S(2)}) %collective-permute-start.2) | collective-permute-done | bytes 524320 | tf_op jit(solution)/shard_map/ppermute | solution.py:156
  76.0 2.9 %collective-permute-done.3 = bf16[256,2,1024]{2,0,1:T(8,128)(2,1)S(1)} collective-permute-done((bf16[256,2,1024]{2,0,1:T(8,128)(2,1)}, bf16[256,2,1024]{2,0,1:T(8,128)(2,1)S(1)}, u32[]{:S(2)}, u32[]{:S(2)}) %collective-permute-start.3) | collective-permute-done | bytes 1048608 | tf_op jit(solution)/shard_map/ppermute | solution.py:156
  79.2 2.6 %copy.136 = bf16[256,2,2,1024]{0,3,2,1:T(8,128)(2,1)} copy(bf16[256,2,2,1024]{3,0,1,2:T(8,128)(2,1)S(1)} %pad_maximum_fusion) | data formatting | bytes 4194304 | tf_op jit(solution)/shard_map/stack | solution.py:159
  81.8 8.8 %fusion.43 = f32[256,2048]{1,0:T(8,128)S(1)} fusion(bf16[256,4096]{0,1:T(8,128)(2,1)} %bitcast.124, bf16[2048,4096]{1,0:T(8,128)(2,1)} %bitcast.112), kind=kOutput, calls=%fused_computation.80 | convolution fusion | flops 4294967296 | bytes 20971520 | tf_op jit(solution)/shard_map/dot_general | solution.py:320
  91.5 17.8 %exchange1.1 = bf16[8,32,1024]{2,1,0:T(8,128)(2,1)} custom-call(bf16[8,32,1024]{2,1,0:T(8,128)(2,1)} %bitcast.130), custom_call_target="tpu_custom_call" | custom-call | tf_op jit(solution)/shard_map/exchange1/pallas_call | solution.py:67
  110.6 5.3 %multiply_reduce_fusion = (f32[]{:T(128)}, f32[1024,16,128]{2,0,1:T(8,128)S(1)}) fusion(f32[1024,16]{0,1:T(8,128)S(1)} %convert_element_type.149, f32[1024,16]{0,1:T(8,128)S(1)} %convert_element_type.148, bf16[256,128,1]{1,0,2:T(8,128)(2,1)S(1)} %bitcast.109, bf16[16,256]{1,0:T(8,128)(2,1)S(1)} %get-tuple-element.25, bf16[1024,256]{1,0:T(8,128)(2,1)S(1)} %bitcast.105), kind=kOutput, calls=%fused_computation.6 | convolution fusion | flops 1101004800 | bytes 9117700 | tf_op jit(solution)/shard_map/dot_general | solution.py:183
  115.9 7.5 %fusion.21 = bf16[16,16,1024]{2,0,1:T(8,128)(2,1)S(1)} fusion(bf16[16,128,1]{1,0,2:T(8,128)(2,1)S(1)} %bitcast.143, f32[1024,16]{0,1:T(8,128)S(1)} %convert_element_type.149, f32[1024,16]{0,1:T(8,128)S(1)} %convert_element_type.148, f32[1024,16,128]{2,0,1:T(8,128)S(1)} %get-tuple-element.31), kind=kOutput, calls=%fused_computation.25 | convolution fusion | flops 90439680 | bytes 9048064 | tf_op jit(solution)/shard_map/ast,kt->ksa/dot_general | solution.py:167
  124.5 17.4 %exchange2.1 = bf16[8,32,1024]{2,1,0:T(8,128)(2,1)} custom-call(bf16[8,32,1024]{2,1,0:T(8,128)(2,1)} %bitcast.135), custom_call_target="tpu_custom_call" | custom-call | tf_op jit(solution)/shard_map/exchange2/pallas_call | solution.py:67
  143.8 11.5 %adjoint.3 = bf16[4,256,1024]{2,1,0:T(8,128)(2,1)} custom-call(bf16[256,1024]{1,0:T(8,128)(2,1)} %bitcast.122, bf16[2,1024,4096]{2,1,0:T(8,128)(2,1)} %bitcast.113), custom_call_target="tpu_custom_call" | custom-call | flops 4294967296 | bytes 19398656 | tf_op jit(solution)/shard_map/adjoint/pallas_call | solution.py:214
  157.7 7.6 %all-to-all-start.2 = ((bf16[8,32,1024]{2,1,0:T(8,128)(2,1)}), bf16[8,32,1024]{2,1,0:T(8,128)(2,1)S(1)}, u32[]{:S(2)}, u32[]{:S(2)}) async-start(bf16[8,32,1024]{2,1,0:T(8,128)(2,1)} %bitcast.21), calls=%async_computation.2 | async-start | bytes 1048576 | tf_op jit(solution)/shard_map/all_to_all | solution.py:337
  165.3 2.0 fusion.12
  170.3 10.1 %all-to-all-done.2 = bf16[8,32,1024]{2,1,0:T(8,128)(2,1)S(1)} async-done(((bf16[8,32,1024]{2,1,0:T(8,128)(2,1)}), bf16[8,32,1024]{2,1,0:T(8,128)(2,1)S(1)}, u32[]{:S(2)}, u32[]{:S(2)}) %all-to-all-start.2) | async-done | bytes 524320 | tf_op jit(solution)/shard_map/all_to_all | solution.py:337
  184.5 14.0 %exchange3.1 = bf16[8,32,1024]{2,1,0:T(8,128)(2,1)} custom-call(bf16[8,32,1024]{2,1,0:T(8,128)(2,1)} %bitcast.137), custom_call_target="tpu_custom_call" | custom-call | tf_op jit(solution)/shard_map/exchange3/pallas_call | solution.py:67
  199.8 2.3 fusion.23
  202.1 2.2 multiply_reduce_fusion.1
  204.3 2.6 %pad_maximum_fusion.2 = f32[4]{0:T(128)S(1)} fusion(f32[1]{0:T(128)} %bitcast.56, f32[1]{0:T(128)} %bitcast.55, f32[1]{0:T(128)} %bitcast.41, f32[1]{0:T(128)} %bitcast.23), kind=kLoop, calls=%fused_computation.72 | loop fusion | flops 12 | bytes 32 | tf_op jit(solution)/shard_map/stack | solution.py:375
  207.6 13.0 %total4.1.sums_ref = f32[8,128]{1,0:T(8,128)} custom-call(f32[8,128]{1,0:T(8,128)} %broadcast_in_dim.8.x_ref), custom_call_target="tpu_custom_call" | custom-call | tf_op jit(solution)/shard_map/total4/pallas_call | solution.py:114
  221.3 15.7 %final.1 = (f32[1024,16,128]{2,1,0:T(8,128)}, f32[1024,16,128]{2,1,0:T(8,128)}, f32[1024,16,128]{2,1,0:T(8,128)}) custom-call(f32[8,128]{1,0:T(8,128)S(1)} %copy-done, f32[1024,16,128]{2,1,0:T(8,128)} %rec_ref.1, f32[1024,32]{1,0:T(8,128)S(1)} %copy.146.win_ref, bf16[1024,256]{1,0:T(8,128)(2,1)S(1)} %bitcast.107, bf16[1024,256]{1,0:T(8,128)(2,1)S(1)} %bitcast.106, ...), custom_call_target="tpu_custom_call" | custom-call | flops 4294967296 | bytes 33554432 | tf_op jit(solution)/shard_map/final/pallas_call | solution.py:291
  (60 shorter events, 29.9 us)
Async XLA Ops:
  29.9 18.9 %copy-start.3 = (s32[8]{0:T(128)S(1)}, s32[8]{0:T(128)}, u32[]{:S(2)}) copy-start(s32[8]{0:T(128)} %param.9) | copy-start | bytes 100
  42.8 2.7 %collective-permute-start = (bf16[2,256,1024]{2,1,0:T(8,128)(2,1)S(1)}, bf16[2,256,1024]{2,1,0:T(8,128)(2,1)S(1)}, u32[]{:S(2)}, u32[]{:S(2)}) collective-permute-start(bf16[2,256,1024]{2,1,0:T(8,128)(2,1)S(1)} %dynamic-slice_bitcast_fusion.1), channel_id=1, source_target_pairs={{0,1},{1,0},{2,3},{3,2},{4,5},{5,4},{6,7},{7,6},{8,9},{9,8},{10,11... | collective-permute-start | bytes 3145736 | tf_op jit(solution)/shard_map/ppermute | solution.py:143
  47.2 14.0 %collective-permute-start.1 = (bf16[1,256,1024]{2,1,0:T(8,128)(2,1)S(1)}, bf16[1,256,1024]{2,1,0:T(8,128)(2,1)S(1)}, u32[]{:S(2)}, u32[]{:S(2)}) collective-permute-start(bf16[1,256,1024]{2,1,0:T(8,128)(2,1)S(1)} %constant_dynamic-slice_fusion.1), channel_id=1, source_target_pairs={{0,2},{1,3},{2,0},{3,1},{4,6},{5,7},{6,4},{7,5},{8,10},{9,11},{10,... | collective-permute-start | bytes 1572872 | tf_op jit(solution)/shard_map/ppermute | solution.py:143
  61.7 13.2 %collective-permute-start.2 = (bf16[256,1,1024]{2,0,1:T(8,128)(2,1)S(1)}, bf16[256,1,1024]{2,0,1:T(8,128)(2,1)S(1)}, u32[]{:S(2)}, u32[]{:S(2)}) collective-permute-start(bf16[256,1,1024]{2,0,1:T(8,128)(2,1)S(1)} %get-tuple-element.34), channel_id=1, source_target_pairs={{0,2},{1,3},{2,0},{3,1},{4,6},{5,7},{6,4},{7,5},{8,10},{9,11},{10,... | collective-permute-start | bytes 1572872 | tf_op jit(solution)/shard_map/ppermute | solution.py:156
  76.0 2.9 %collective-permute-start.3 = (bf16[256,2,1024]{2,0,1:T(8,128)(2,1)}, bf16[256,2,1024]{2,0,1:T(8,128)(2,1)S(1)}, u32[]{:S(2)}, u32[]{:S(2)}) collective-permute-start(bf16[256,2,1024]{2,0,1:T(8,128)(2,1)} %maximum_bitcast_fusion), channel_id=1, source_target_pairs={{0,1},{1,0},{2,3},{3,2},{4,5},{5,4},{6,7},{7,6},{8,9},{9,8},{10,11... | collective-permute-start | bytes 3145736 | tf_op jit(solution)/shard_map/ppermute | solution.py:156
  155.3 14.3 %copy-start.1 = (s32[1024,16]{0,1:T(8,128)S(1)}, s32[1024,16]{0,1:T(8,128)}, u32[]{:S(2)}) copy-start(s32[1024,16]{0,1:T(8,128)} %param.11) | copy-start | bytes 196612
  155.3 14.3 %copy-start.2 = (s32[1024,16]{0,1:T(8,128)S(1)}, s32[1024,16]{0,1:T(8,128)}, u32[]{:S(2)}) copy-start(s32[1024,16]{0,1:T(8,128)} %param.10) | copy-start | bytes 196612
  156.7 8.6 %collective-permute-start.4 = (bf16[2,256,1024]{2,1,0:T(8,128)(2,1)S(1)}, bf16[2,256,1024]{2,1,0:T(8,128)(2,1)}, u32[]{:S(2)}, u32[]{:S(2)}) collective-permute-start(bf16[2,256,1024]{2,1,0:T(8,128)(2,1)S(1)} %dynamic-slice_bitcast_fusion), channel_id=1, source_target_pairs={{0,1},{1,0},{2,3},{3,2},{4,5},{5,4},{6,7},{7,6},{8,9},{9,8},{10,11... | collective-permute-start | bytes 3145736 | tf_op jit(solution)/shard_map/ppermute | solution.py:143
  157.7 22.7 %all-to-all-start.2 = ((bf16[8,32,1024]{2,1,0:T(8,128)(2,1)}), bf16[8,32,1024]{2,1,0:T(8,128)(2,1)S(1)}, u32[]{:S(2)}, u32[]{:S(2)}) async-start(bf16[8,32,1024]{2,1,0:T(8,128)(2,1)} %bitcast.21), calls=%async_computation.2 | async-start | bytes 1048576 | tf_op jit(solution)/shard_map/all_to_all | solution.py:337
  168.1 14.4 %collective-permute-start.5 = (bf16[1,256,1024]{2,1,0:T(8,128)(2,1)}, bf16[1,256,1024]{2,1,0:T(8,128)(2,1)}, u32[]{:S(2)}, u32[]{:S(2)}) collective-permute-start(bf16[1,256,1024]{2,1,0:T(8,128)(2,1)} %constant_dynamic-slice_fusion), channel_id=1, source_target_pairs={{0,2},{1,3},{2,0},{3,1},{4,6},{5,7},{6,4},{7,5},{8,10},{9,11},{10,... | collective-permute-start | bytes 1572872 | tf_op jit(solution)/shard_map/ppermute | solution.py:143
  220.6 0.7 copy-start

commit v2 on v1

--- a/solution.py
+++ b/solution.py
@@ -79,17 +79,13 @@
     )(x)
 
 
-def total_kernel(outer, inner, x_ref, o_ref, held, send_sem, recv_sem):
-    n = outer * inner
-    me = lax.axis_index("gx") * inner + lax.axis_index("ma")
+def total_kernel(n, axis, x_ref, o_ref, held, send_sem, recv_sem):
+    me = lax.axis_index(axis)
     barrier = pltpu.get_barrier_semaphore()
-
-    def place(k):
-        peer = lax.rem(me + k, n)
-        return (peer // inner, lax.rem(peer, inner))
-
     for k in range(1, n):
-        pl.semaphore_signal(barrier, inc=1, device_id=place(k), device_id_type=MESH)
+        pl.semaphore_signal(
+            barrier, inc=1, device_id={axis: lax.rem(me + k, n)}, device_id_type=MESH
+        )
     pl.semaphore_wait(barrier, n - 1)
     copies = []
     for k in range(1, n):
@@ -98,7 +94,7 @@
             dst_ref=held.at[me],
             send_sem=send_sem.at[k],
             recv_sem=recv_sem.at[k],
-            device_id=place(k),
+            device_id={axis: lax.rem(me + k, n)},
             device_id_type=MESH,
         )
         copy.start()
@@ -109,10 +105,9 @@
     o_ref[...] = jnp.sum(held[...], axis=0)
 
 
-def total(x, outer, inner, number):
-    n = outer * inner
+def total(x, n, axis, number):
     return pl.pallas_call(
-        functools.partial(total_kernel, outer, inner),
+        functools.partial(total_kernel, n, axis),
         out_shape=jax.ShapeDtypeStruct(x.shape, x.dtype),
         in_specs=[pl.BlockSpec(memory_space=pltpu.VMEM)],
         out_specs=pl.BlockSpec(memory_space=pltpu.VMEM),
@@ -149,16 +144,16 @@
 def gather_all(x, n):
     rows, block = x.shape
     me = lax.axis_index("ma")
-    held = x.reshape(rows, 1, block)
+    held = x[None]
     bit = n // 2
     while bit >= 1:
         own = (me // bit) % 2
         got = lax.ppermute(held, "ma", pairs(n, bit))
         first = jnp.where(own == 0, held, got)
         second = jnp.where(own == 0, got, held)
-        held = jnp.stack([first, second], 2).reshape(rows, -1, block)
+        held = jnp.stack([first, second], 1).reshape(-1, rows, block)
         bit //= 2
-    return held.reshape(rows, n * block)
+    return held
 
 
 def to_spectra(traces, table):
@@ -314,16 +309,49 @@
     )(sums, recorded, window, across(returned), across(arrived), across(changed), tall, mask, pick)
 
 
+def forward_kernel(n, x_ref, k_ref, o_ref):
+    half = x_ref.shape[1] // 2
+    block = x_ref.shape[2]
+    totals = []
+    for part in range(2):
+        total_part = None
+        for i in range(n):
+            term = lax.dot_general(
+                x_ref[i],
+                k_ref[part, :, i * block : (i + 1) * block],
+                (((1,), (1,)), ((), ())),
+                preferred_element_type=jnp.float32,
+            )
+            total_part = term if total_part is None else total_part + term
+        totals.append(total_part)
+    first, second = totals
+    o_ref[:half] = (first[:half] - second[half:]).astype(o_ref.dtype)
+    o_ref[half:] = (first[half:] + second[:half]).astype(o_ref.dtype)
+
+
 def forward_product(model, flat_kernel, inner):
     sources = model.shape[1]
     incoming = gather_all(model.reshape(2 * sources, -1), inner)
-    product = lax.dot_general(
-        incoming, flat_kernel, (((1,), (1,)), ((), ())), preferred_element_type=jnp.float32
-    )
-    half = flat_kernel.shape[0] // 2
-    real_part = product[:sources, :half] - product[sources:, half:]
-    imaginary = product[sources:, :half] + product[:sources, half:]
-    return jnp.stack([real_part, imaginary], 0).astype(jnp.bfloat16)
+    rows, columns = flat_kernel.shape[0] // 2, flat_kernel.shape[1]
+    tile = min(256, rows)
+    product = pl.pallas_call(
+        functools.partial(forward_kernel, inner),
+        grid=(rows // tile,),
+        out_shape=jax.ShapeDtypeStruct((2 * sources, rows), jnp.bfloat16),
+        in_specs=[
+            pl.BlockSpec(incoming.shape, lambda j: (0, 0, 0)),
+            pl.BlockSpec((2, tile, columns), lambda j: (0, j, 0)),
+        ],
+        out_specs=pl.BlockSpec((2 * sources, tile), lambda j: (0, j)),
+        compiler_params=pltpu.CompilerParams(vmem_limit_bytes=60 * 1024 * 1024),
+        cost_estimate=pl.CostEstimate(
+            flops=8 * sources * rows * columns,
+            bytes_accessed=4 * rows * columns + 4 * sources * (rows + columns),
+            transcendentals=0,
+        ),
+        name="forward",
+    )(incoming, flat_kernel.reshape(2, rows, columns))
+    return product.reshape(2, sources, rows)
 
 
 def per_device(outer, inner, recorded, kernel, freq_bins, window_start, window_stop):
@@ -334,27 +362,21 @@
 
     data = by_frequency(exchange(to_spectra(weights * recorded, table), outer, 0), outer)
     adjoint = adjoint_product(data, flat_kernel, inner)
-    returned = lax.all_to_all(
-        by_source(adjoint, outer), "gx", split_axis=0, concat_axis=0, tiled=True
-    )
+    returned = exchange(by_source(adjoint, outer), outer, 6)
 
     same = freq_bins[:, None] == freq_bins[None, :]
     repeated = jnp.sum(same.astype(jnp.int32)) > freq_bins.shape[0]
 
-    def combined(spectra):
-        parts = lax.all_to_all(
-            by_source(spectra, outer), "gx", split_axis=0, concat_axis=0, tiled=True
-        )
+    def combined(spectra, parts):
         mixed = jnp.einsum(
             "gf,fxa->gxa",
             same.astype(jnp.bfloat16),
             parts,
             preferred_element_type=jnp.float32,
         ).astype(jnp.bfloat16)
-        back = lax.all_to_all(mixed, "gx", split_axis=0, concat_axis=0, tiled=True)
-        return by_frequency(back, outer)
-
-    model = lax.cond(repeated, combined, lambda spectra: spectra, adjoint)
+        return by_frequency(exchange(mixed, outer, 7), outer)
+
+    model = lax.cond(repeated, combined, lambda spectra, parts: spectra, adjoint, returned)
     outgoing = by_source(forward_product(model, flat_kernel, inner), outer)
     imaged = exchange(outgoing, outer, 1)
     image = weights * to_traces(imaged, table)
@@ -380,7 +402,8 @@
             jnp.sum(flat_h.astype(jnp.float32) * mixed_h),
         ]
     )
-    sums = total(jnp.broadcast_to(jnp.tile(sums, 2)[:, None], (8, 128)), outer, inner, 4)
+    sums = jnp.broadcast_to(jnp.tile(sums, 2)[:, None], (8, 128))
+    sums = total(total(sums, inner, "ma", 4), outer, "gx", 5)
     if recorded.shape[1] % 8 == 0:
         return tuple(
             final_step(

time: 239 us -> 254 us (1.063)
  Pallas kernels: 117 us -> 147 us
  matrix products: 33.4 us -> 24.5 us
  starting transfers between devices: 12.4 us -> 4.82 us
    pallas_call x4 -> x5, Pallas kernels: 65.6 us -> 82.7 us  [exchange(): pl.pallas_call(functools.partial(exchange_kernel, n), out_shape=jax.Shape...]
    pallas_call x1 -> x3, Pallas kernels: 13 us -> 25.7 us  [the longest x2 15.8 us: total(): pl.pallas_call(functools.partial(total_kernel, n, axis), out_shape=jax.Sh...]
    ppermute x4, waiting for transfers between devices: 15.4 us -> 28 us  [scatter_sum(): got = lax.ppermute(send, 'ma', pairs(n, bit))]
    all_to_all x1 -> x0, waiting for transfers between devices: 10.1 us -> none  [per_device(): lax.all_to_all(by_source(adjoint, outer), 'gx', split_axis=0, concat_axis...]
    dot_general x1 -> x0, matrix products: 8.78 us -> none  [forward_product(): lax.dot_general(incoming, flat_kernel, (((1,), (1,)), ((), ())), preferre...]
    all_to_all x1 -> x0, starting transfers between devices: 7.57 us -> none  [per_device(): lax.all_to_all(by_source(adjoint, outer), 'gx', split_axis=0, concat_axis...]
  transfers between devices with their start and end apart: 7 -> 6, of which waited for: 6 -> 6; matrix products, arithmetic and copies ran while one was open for 2% -> 1% of each run, Pallas kernels for 0% -> 0%
where the time goes in v2:
time: 254 us; the launch traced here: 252 us
  Pallas kernels  147 us (58%)
  waiting for transfers between devices  42.4 us (17%)
  matrix products  24.5 us (10%)
  local copies, waits for them, and re-layouts  19.2 us (8%)
  other arithmetic  12.3 us (5%)
  starting transfers between devices  4.82 us (2%)
    pallas_call x5, Pallas kernels, exchange(): pl.pallas_call(functools.partial(exchange_kernel, n), out_shape=jax.Shape...  82.7 us
    ppermute x4, waiting for transfers between devices, scatter_sum(): got = lax.ppermute(send, 'ma', pairs(n, bit))  28 us
    pallas_call x2, Pallas kernels, adjoint_product(): pl.pallas_call(adjoint_kernel, grid=(columns // tile,), out_shape=jax.Sha...  23.2 us
    pallas_call x2, Pallas kernels, total(): pl.pallas_call(functools.partial(total_kernel, n, axis), out_shape=jax.Sh...  15.8 us
    pallas_call x1, Pallas kernels, final_step(): pl.pallas_call(final_kernel, grid=(points // tile,), out_shape=[jax.Shape...  15.7 us
    dot_general x2, matrix products, to_spectra(): jnp.einsum('ast,kt->ksa', traces.astype(jnp.bfloat16), flat, preferred_el...  14.9 us
    ppermute x2, waiting for transfers between devices, gather_all(): got = lax.ppermute(held, 'ma', pairs(n, bit))  14.3 us
    pallas_call x1, Pallas kernels, forward_product(): pl.pallas_call(functools.partial(forward_kernel, inner), grid=(rows // ti...  9.89 us
  transfers between devices with their start and end apart: 6, of which 6 were waited for; matrix products, arithmetic and copies ran while one was open for 1% of the time, Pallas kernels for 0%

profile of v2, /device:TPU:0, one launch (start us, length us, event | category | flops | bytes accessed | tf_op | source)
XLA Modules:
  0.0 252.3 jit_solution(2747039411321086383)
XLA Ops:
  3.1 7.4 %fusion.19 = bf16[16,16,1024]{2,0,1:T(8,128)(2,1)S(1)} fusion(bf16[16,128,1]{1,0,2:T(8,128)(2,1)S(1)} %bitcast.125, f32[1024,16,128]{2,1,0:T(8,128)} %rec_ref.1, f32[1024,16]{0,1:T(8,128)S(1)} %convert_element_type.147, f32[1024,16]{0,1:T(8,128)S(1)} %convert_element_type.146), kind=kOutput, calls=%fused_computation.25 | convolution fusion | flops 88342528 | bytes 9048064 | tf_op jit(solution)/shard_map/ast,kt->ksa/dot_general | solution.py:162
  11.6 16.4 %exchange0.1 = bf16[8,32,1024]{2,1,0:T(8,128)(2,1)} custom-call(bf16[8,32,1024]{2,1,0:T(8,128)(2,1)} %bitcast.117), custom_call_target="tpu_custom_call" | custom-call | tf_op jit(solution)/shard_map/exchange0/pallas_call | solution.py:67
  28.0 1.9 copy.88
  29.9 11.6 %adjoint.2 = bf16[4,256,1024]{2,1,0:T(8,128)(2,1)} custom-call(bf16[256,1024]{1,0:T(8,128)(2,1)} %bitcast.110, bf16[2,1024,4096]{2,1,0:T(8,128)(2,1)} %bitcast.98), custom_call_target="tpu_custom_call" | custom-call | flops 4294967296 | bytes 19398656 | tf_op jit(solution)/shard_map/adjoint/pallas_call | solution.py:209
  42.9 2.6 %collective-permute-done = bf16[2,256,1024]{2,1,0:T(8,128)(2,1)S(1)} collective-permute-done((bf16[2,256,1024]{2,1,0:T(8,128)(2,1)S(1)}, bf16[2,256,1024]{2,1,0:T(8,128)(2,1)S(1)}, u32[]{:S(2)}, u32[]{:S(2)}) %collective-permute-start) | collective-permute-done | bytes 1048608 | tf_op jit(solution)/shard_map/ppermute | solution.py:138
  50.2 11.0 %collective-permute-done.1 = bf16[1,256,1024]{2,1,0:T(8,128)(2,1)S(1)} collective-permute-done((bf16[1,256,1024]{2,1,0:T(8,128)(2,1)S(1)}, bf16[1,256,1024]{2,1,0:T(8,128)(2,1)S(1)}, u32[]{:S(2)}, u32[]{:S(2)}) %collective-permute-start.1) | collective-permute-done | bytes 524320 | tf_op jit(solution)/shard_map/ppermute | solution.py:138
  62.2 16.1 %exchange6.1 = bf16[8,32,1024]{2,1,0:T(8,128)(2,1)S(1)} custom-call(bf16[8,32,1024]{2,1,0:T(8,128)(2,1)} %bitcast.124), custom_call_target="tpu_custom_call" | custom-call | tf_op jit(solution)/shard_map/exchange6/pallas_call | solution.py:67
  80.1 11.5 %collective-permute-done.2 = bf16[1,256,1024]{2,1,0:T(8,128)(2,1)S(1)} collective-permute-done((bf16[1,256,1024]{2,1,0:T(8,128)(2,1)S(1)}, bf16[1,256,1024]{2,1,0:T(8,128)(2,1)S(1)}, u32[]{:S(2)}, u32[]{:S(2)}) %collective-permute-start.2) | collective-permute-done | bytes 524320 | tf_op jit(solution)/shard_map/ppermute | solution.py:151
  92.7 2.9 %collective-permute-done.3 = bf16[2,256,1024]{2,1,0:T(8,128)(2,1)S(1)} collective-permute-done((bf16[2,256,1024]{2,1,0:T(8,128)(2,1)}, bf16[2,256,1024]{2,1,0:T(8,128)(2,1)S(1)}, u32[]{:S(2)}, u32[]{:S(2)}) %collective-permute-start.3) | collective-permute-done | bytes 1048608 | tf_op jit(solution)/shard_map/ppermute | solution.py:151
  97.4 9.9 %forward.1 = bf16[256,1024]{1,0:T(8,128)(2,1)} custom-call(bf16[4,256,1024]{2,1,0:T(8,128)(2,1)} %bitcast.105, bf16[2,1024,4096]{2,1,0:T(8,128)(2,1)} %bitcast.99), custom_call_target="tpu_custom_call" | custom-call | flops 4294967296 | bytes 19398656 | tf_op jit(solution)/shard_map/forward/pallas_call | solution.py:337
  109.2 18.1 %exchange1.1 = bf16[8,32,1024]{2,1,0:T(8,128)(2,1)} custom-call(bf16[8,32,1024]{2,1,0:T(8,128)(2,1)} %bitcast.119), custom_call_target="tpu_custom_call" | custom-call | tf_op jit(solution)/shard_map/exchange1/pallas_call | solution.py:67
  128.6 5.2 %multiply_reduce_fusion = (f32[]{:T(128)}, f32[1024,16,128]{2,0,1:T(8,128)S(1)}) fusion(f32[1024,16]{0,1:T(8,128)S(1)} %convert_element_type.147, f32[1024,16]{0,1:T(8,128)S(1)} %convert_element_type.146, bf16[256,128,1]{1,0,2:T(8,128)(2,1)S(1)} %bitcast.96, bf16[16,256]{1,0:T(8,128)(2,1)S(1)} %get-tuple-element.33, bf16[1024,256]{1,0:T(8,128)(2,1)S(1)} %bitcast.92), kind=kOutput, calls=%fused_computation.7 | convolution fusion | flops 1101004800 | bytes 9117700 | tf_op jit(solution)/shard_map/dot_general | solution.py:178
  133.8 7.5 %fusion.22 = bf16[16,16,1024]{2,0,1:T(8,128)(2,1)S(1)} fusion(bf16[16,128,1]{1,0,2:T(8,128)(2,1)S(1)} %bitcast.127, f32[1024,16]{0,1:T(8,128)S(1)} %convert_element_type.147, f32[1024,16]{0,1:T(8,128)S(1)} %convert_element_type.146, f32[1024,16,128]{2,0,1:T(8,128)S(1)} %get-tuple-element.39), kind=kOutput, calls=%fused_computation.26 | convolution fusion | flops 90439680 | bytes 9048064 | tf_op jit(solution)/shard_map/ast,kt->ksa/dot_general | solution.py:162
  142.4 15.9 %exchange2.1 = bf16[8,32,1024]{2,1,0:T(8,128)(2,1)} custom-call(bf16[8,32,1024]{2,1,0:T(8,128)(2,1)} %bitcast.121), custom_call_target="tpu_custom_call" | custom-call | tf_op jit(solution)/shard_map/exchange2/pallas_call | solution.py:67
  160.2 11.6 %adjoint.3 = bf16[4,256,1024]{2,1,0:T(8,128)(2,1)} custom-call(bf16[256,1024]{1,0:T(8,128)(2,1)} %bitcast.112, bf16[2,1024,4096]{2,1,0:T(8,128)(2,1)} %bitcast.100), custom_call_target="tpu_custom_call" | custom-call | flops 4294967296 | bytes 19398656 | tf_op jit(solution)/shard_map/adjoint/pallas_call | solution.py:209
  173.3 2.5 collective-permute-done.4
  180.7 11.9 %collective-permute-done.5 = bf16[1,256,1024]{2,1,0:T(8,128)(2,1)} collective-permute-done((bf16[1,256,1024]{2,1,0:T(8,128)(2,1)}, bf16[1,256,1024]{2,1,0:T(8,128)(2,1)}, u32[]{:S(2)}, u32[]{:S(2)}) %collective-permute-start.5) | collective-permute-done | bytes 524320 | tf_op jit(solution)/shard_map/ppermute | solution.py:138
  194.7 16.2 %exchange3.1 = bf16[8,32,1024]{2,1,0:T(8,128)(2,1)} custom-call(bf16[8,32,1024]{2,1,0:T(8,128)(2,1)} %bitcast.123), custom_call_target="tpu_custom_call" | custom-call | tf_op jit(solution)/shard_map/exchange3/pallas_call | solution.py:67
  210.9 2.2 multiply_reduce_fusion.1
  213.1 2.2 fusion.24
  216.6 2.7 %pad_maximum_fusion.1 = f32[4]{0:T(128)S(1)} fusion(f32[1]{0:T(128)} %bitcast.48, f32[1]{0:T(128)} %bitcast.47, f32[1]{0:T(128)} %bitcast.33, f32[1]{0:T(128)} %bitcast.19), kind=kLoop, calls=%fused_computation.68 | loop fusion | flops 12 | bytes 32 | tf_op jit(solution)/shard_map/stack | solution.py:397
  220.0 5.0 %total4.1.x_ref = f32[8,128]{1,0:T(8,128)} custom-call(f32[8,128]{1,0:T(8,128)} %broadcast_in_dim.8.x_ref), custom_call_target="tpu_custom_call" | custom-call | tf_op jit(solution)/shard_map/total4/pallas_call | solution.py:109
  225.0 10.9 %total5.1.sums_ref = f32[8,128]{1,0:T(8,128)} custom-call(f32[8,128]{1,0:T(8,128)} %total4.1.x_ref), custom_call_target="tpu_custom_call" | custom-call | tf_op jit(solution)/shard_map/total5/pallas_call | solution.py:109
  236.6 15.7 %final.1 = (f32[1024,16,128]{2,1,0:T(8,128)}, f32[1024,16,128]{2,1,0:T(8,128)}, f32[1024,16,128]{2,1,0:T(8,128)}) custom-call(f32[8,128]{1,0:T(8,128)S(1)} %copy-done, f32[1024,16,128]{2,1,0:T(8,128)} %rec_ref.1, f32[1024,32]{1,0:T(8,128)S(1)} %copy.101.win_ref, bf16[1024,256]{1,0:T(8,128)(2,1)S(1)} %bitcast.94, bf16[1024,256]{1,0:T(8,128)(2,1)S(1)} %bitcast.93, ...), custom_call_target="tpu_custom_call" | custom-call | flops 4294967296 | bytes 33554432 | tf_op jit(solution)/shard_map/final/pallas_call | solution.py:286
  (58 shorter events, 31.9 us)
Async XLA Ops:
  29.9 18.9 %copy-start.3 = (s32[8]{0:T(128)S(1)}, s32[8]{0:T(128)}, u32[]{:S(2)}) copy-start(s32[8]{0:T(128)} %param.9) | copy-start | bytes 100
  42.8 2.7 %collective-permute-start = (bf16[2,256,1024]{2,1,0:T(8,128)(2,1)S(1)}, bf16[2,256,1024]{2,1,0:T(8,128)(2,1)S(1)}, u32[]{:S(2)}, u32[]{:S(2)}) collective-permute-start(bf16[2,256,1024]{2,1,0:T(8,128)(2,1)S(1)} %dynamic-slice_bitcast_fusion.1), channel_id=1, source_target_pairs={{0,1},{1,0},{2,3},{3,2},{4,5},{5,4},{6,7},{7,6},{8,9},{9,8},{10,11... | collective-permute-start | bytes 3145736 | tf_op jit(solution)/shard_map/ppermute | solution.py:138
  47.2 14.0 %collective-permute-start.1 = (bf16[1,256,1024]{2,1,0:T(8,128)(2,1)S(1)}, bf16[1,256,1024]{2,1,0:T(8,128)(2,1)S(1)}, u32[]{:S(2)}, u32[]{:S(2)}) collective-permute-start(bf16[1,256,1024]{2,1,0:T(8,128)(2,1)S(1)} %constant_dynamic-slice_fusion.1), channel_id=1, source_target_pairs={{0,2},{1,3},{2,0},{3,1},{4,6},{5,7},{6,4},{7,5},{8,10},{9,11},{10,... | collective-permute-start | bytes 1572872 | tf_op jit(solution)/shard_map/ppermute | solution.py:138
  78.5 13.1 %collective-permute-start.2 = (bf16[1,256,1024]{2,1,0:T(8,128)(2,1)S(1)}, bf16[1,256,1024]{2,1,0:T(8,128)(2,1)S(1)}, u32[]{:S(2)}, u32[]{:S(2)}) collective-permute-start(bf16[1,256,1024]{2,1,0:T(8,128)(2,1)S(1)} %get-tuple-element.42), channel_id=1, source_target_pairs={{0,2},{1,3},{2,0},{3,1},{4,6},{5,7},{6,4},{7,5},{8,10},{9,11},{10,... | collective-permute-start | bytes 1572872 | tf_op jit(solution)/shard_map/ppermute | solution.py:151
  92.7 2.9 %collective-permute-start.3 = (bf16[2,256,1024]{2,1,0:T(8,128)(2,1)}, bf16[2,256,1024]{2,1,0:T(8,128)(2,1)S(1)}, u32[]{:S(2)}, u32[]{:S(2)}) collective-permute-start(bf16[2,256,1024]{2,1,0:T(8,128)(2,1)} %maximum_bitcast_fusion), channel_id=1, source_target_pairs={{0,1},{1,0},{2,3},{3,2},{4,5},{5,4},{6,7},{7,6},{8,9},{9,8},{10,11... | collective-permute-start | bytes 3145736 | tf_op jit(solution)/shard_map/ppermute | solution.py:151
  160.2 19.6 %copy-start.1 = (s32[1024,16]{0,1:T(8,128)S(1)}, s32[1024,16]{0,1:T(8,128)}, u32[]{:S(2)}) copy-start(s32[1024,16]{0,1:T(8,128)} %param.11) | copy-start | bytes 196612
  160.2 19.6 %copy-start.2 = (s32[1024,16]{0,1:T(8,128)S(1)}, s32[1024,16]{0,1:T(8,128)}, u32[]{:S(2)}) copy-start(s32[1024,16]{0,1:T(8,128)} %param.10) | copy-start | bytes 196612
  173.1 2.7 %collective-permute-start.4 = (bf16[2,256,1024]{2,1,0:T(8,128)(2,1)S(1)}, bf16[2,256,1024]{2,1,0:T(8,128)(2,1)S(1)}, u32[]{:S(2)}, u32[]{:S(2)}) collective-permute-start(bf16[2,256,1024]{2,1,0:T(8,128)(2,1)S(1)} %dynamic-slice_bitcast_fusion), channel_id=1, source_target_pairs={{0,1},{1,0},{2,3},{3,2},{4,5},{5,4},{6,7},{7,6},{8,9},{9,8},{10,11... | collective-permute-start | bytes 3145736 | tf_op jit(solution)/shard_map/ppermute | solution.py:138
  178.3 14.3 %collective-permute-start.5 = (bf16[1,256,1024]{2,1,0:T(8,128)(2,1)}, bf16[1,256,1024]{2,1,0:T(8,128)(2,1)}, u32[]{:S(2)}, u32[]{:S(2)}) collective-permute-start(bf16[1,256,1024]{2,1,0:T(8,128)(2,1)} %constant_dynamic-slice_fusion), channel_id=1, source_target_pairs={{0,2},{1,3},{2,0},{3,1},{4,6},{5,7},{6,4},{7,5},{8,10},{9,11},{10,... | collective-permute-start | bytes 1572872 | tf_op jit(solution)/shard_map/ppermute | solution.py:138
  235.9 0.7 copy-start
